TPU v7x, 128 devices: a whole 4x4x4 slice. The times are simulated.
128 devices in a mesh: blk: 8 (over x, z_hi), grp: 16 (over z_lo, y, core).
Axes of the slice: x: 4, y: 4, z: 4 (z_hi: 2, z_lo: 2; z = z_hi * 2 + z_lo), core: 2. Of those that a mesh axis runs over, the one named last changes fastest.
Arguments:
- frames: bfloat16 [16384, 8, 2048], P(('blk', 'grp')), may hold values from -6 to 6
- counts: int32 [16384], P(('blk', 'grp')), may hold values from 1 to 8
- positives: int32 [16384], P(('blk', 'grp')), may hold values from 0 to 16383, as said below
- w_first: bfloat16 [2048, 4096], P(None, 'grp'), may hold values from -0.125 to 0.125
- w_second: bfloat16 [4096, 256], P('grp'), may hold values from -0.09375 to 0.09375
Outputs:
- batch_loss: float32 [], replicated
- grad_first: float32 [2048, 4096], P(None, 'grp')
- grad_second: float32 [4096, 256], P('grp')
Inputs may be any that keep to these rules, and one draw needn't show every extreme that they name: positives[positives[i]] = i and positives[i] != i for every clip i.
All inputs are finite; a program needn't handle non-finite values.
Results may differ from a plain program's by a relative error of at most 0.005.
The roundings to bfloat16 on the way count: a program that leaves them out, or rounds other values in their place, can miss the bound.
Values may be sent and summed in bfloat16 or wider, within the bound.
No kernel may reach another device: no remote copies, remote signals or barrier semaphores. Data moves between devices by JAX's collectives and lax.ppermute only.
A program may use at most 128 MiB of HBM per device.

v0:
```python
import jax
import jax.numpy as jnp
from jax import lax
from jax.sharding import Mesh
from jax.sharding import PartitionSpec as P

BLK = ("blk_0", "blk_1")
GRP = ("grp_0", "grp_1", "grp_2")
BLK_GRP = ("blk_0", "blk_1", "grp_0", "grp_1", "grp_2")
logit_sharpness_divisor = 0.05
score_top = 20.0


def in_blocks(array, dim, peers):
    shape = array.shape
    pieces = array.reshape(*shape[:dim], peers, shape[dim] // peers, *shape[dim + 1 :])
    return jnp.moveaxis(pieces, dim, 0)


def sent_and_summed(array, axis, dim):
    peers = lax.axis_size(axis)
    pieces = lax.all_to_all(in_blocks(array, dim, peers), axis, 0, 0, tiled=True)
    return jnp.sum(pieces, axis=0)


def in_order(pieces, dim):
    shape = list(pieces.shape[1:])
    shape[dim] *= pieces.shape[0]
    return jnp.moveaxis(pieces, 0, dim).reshape(shape)


def from_everyone(array, axis):
    peers = lax.axis_size(axis)
    return lax.all_to_all(
        jnp.broadcast_to(array[None], (peers, *array.shape)), axis, 0, 0, tiled=True
    )


def gather_directly(array, axis, dim):
    return in_order(from_everyone(array, axis), dim)


def shifted(block, axis, distance):
    devices = range(lax.axis_size(axis))
    route = [((i - distance) % len(devices), i) for i in devices]
    return lax.ppermute(block, axis, route)


def by_axis(array, axes):
    for axis in axes:
        array = lax.psum(array, axis)
    return array


def shards(frames, counts, positives, w_first, w_second):
    row_count = frames.shape[0]
    slot_count = frames.shape[1]
    cycle_size = lax.axis_size(BLK)
    group_size = lax.axis_size(GRP)
    complete_segment_entries = row_count * cycle_size * group_size
    group_rows = row_count * group_size
    cycle_index = lax.axis_index(BLK)
    first_row = (cycle_index * group_size + lax.axis_index(GRP)) * row_count
    row_ids = first_row + jnp.arange(row_count, dtype=jnp.int32)
    frame_mask = (jnp.arange(slot_count, dtype=jnp.int32)[None, :] < counts[:, None]).astype(
        jnp.bfloat16
    )
    summed = jnp.einsum("rf,rfc->rc", frame_mask, frames, preferred_element_type=jnp.float32)
    pooled = (summed / counts[:, None].astype(jnp.float32)).astype(jnp.bfloat16)
    pooled_all = lax.all_gather(pooled, GRP, axis=0, tiled=True)
    preact = jnp.dot(pooled_all, w_first, preferred_element_type=jnp.float32)
    hidden = jax.nn.gelu(preact).astype(jnp.bfloat16)
    raw_keys = sent_and_summed(
        jnp.dot(hidden, w_second, preferred_element_type=jnp.float32), GRP, 0
    )
    key_length = jnp.sqrt(jnp.sum(raw_keys * raw_keys, axis=1, keepdims=True) + 1e-06)
    unit_keys = raw_keys / key_length
    lower_match_vectors = unit_keys.astype(jnp.bfloat16)
    key_block = gather_directly(lower_match_vectors, GRP, 0)
    block_ids = jnp.arange(group_rows, dtype=jnp.int32)
    exp_total = jnp.zeros((row_count,), jnp.float32)
    pos_score = jnp.zeros((row_count,), jnp.float32)
    stored = []
    for hop_index in range(cycle_size):
        owner = (cycle_index - hop_index) % cycle_size
        offset = owner * group_rows
        key_ids = offset + block_ids
        cosine_logit_matrix = (
            lax.dot_general(
                lower_match_vectors,
                key_block,
                (((1,), (1,)), ((), ())),
                preferred_element_type=jnp.float32,
            )
            / logit_sharpness_divisor
        )
        self_mask = key_ids[None, :] == row_ids[:, None]
        pair_mask = key_ids[None, :] == positives[:, None]
        exp_total = exp_total + jnp.sum(
            jnp.where(self_mask, 0.0, jnp.exp(cosine_logit_matrix - score_top)), axis=1
        )
        pos_score = pos_score + jnp.sum(jnp.where(pair_mask, cosine_logit_matrix, 0.0), axis=1)
        stored.append((key_block, offset, cosine_logit_matrix, self_mask, pair_mask))
        if hop_index + 1 < cycle_size:
            key_block = shifted(key_block, BLK, 1)
    log_norm = jnp.log(exp_total) + score_top
    batch_loss = by_axis(jnp.sum(log_norm - pos_score), BLK_GRP) / complete_segment_entries
    query_gradient = jnp.zeros((row_count, lower_match_vectors.shape[1]), jnp.float32)
    every_norm = lax.all_gather(log_norm, BLK_GRP, axis=0, tiled=True)
    self_key_gradient = jnp.zeros((row_count, lower_match_vectors.shape[1]), jnp.float32)
    for key_block, offset, cosine_logit_matrix, self_mask, pair_mask in stored:
        pair_float = pair_mask.astype(jnp.float32)
        probs = jnp.where(self_mask, 0.0, jnp.exp(cosine_logit_matrix - log_norm[:, None]))
        weights = (probs - pair_float).astype(jnp.bfloat16)
        column_norm = lax.dynamic_slice_in_dim(every_norm, offset, group_rows, 0)
        mirrored = jnp.where(self_mask, 0.0, jnp.exp(cosine_logit_matrix - column_norm[None, :]))
        mirror_weights = (mirrored - pair_float).astype(jnp.bfloat16)
        query_gradient = query_gradient + jnp.dot(
            weights, key_block, preferred_element_type=jnp.float32
        )
        self_key_gradient = self_key_gradient + jnp.dot(
            mirror_weights, key_block, preferred_element_type=jnp.float32
        )
    sphere_projected_derivative = (query_gradient + self_key_gradient) / (
        complete_segment_entries * logit_sharpness_divisor
    )
    raw_grad = (
        (
            sphere_projected_derivative
            - unit_keys * jnp.sum(unit_keys * sphere_projected_derivative, axis=1, keepdims=True)
        )
        / key_length
    ).astype(jnp.bfloat16)
    group_grad = gather_directly(raw_grad, GRP, 0)
    second_grad = lax.dot_general(
        hidden, group_grad, (((0,), (0,)), ((), ())), preferred_element_type=jnp.float32
    )
    hidden_grad = lax.dot_general(
        group_grad, w_second, (((1,), (1,)), ((), ())), preferred_element_type=jnp.float32
    )
    unused, backward = jax.vjp(jax.nn.gelu, preact)
    preact_grad = backward(hidden_grad)[0].astype(jnp.bfloat16)
    first_grad = lax.dot_general(
        pooled_all, preact_grad, (((0,), (0,)), ((), ())), preferred_element_type=jnp.float32
    )
    first_grad, second_grad = lax.psum((first_grad, second_grad), BLK)
    return (batch_loss, first_grad, second_grad)


def solution(mesh):
    finer = Mesh(mesh.devices.reshape(4, 2, 2, 4, 2), ("blk_0", "blk_1", "grp_0", "grp_1", "grp_2"))
    placed = (P(BLK_GRP, None, None), P(BLK_GRP), P(BLK_GRP), P(None, GRP), P(GRP, None))
    return jax.shard_map(
        shards,
        mesh=finer,
        in_specs=placed,
        out_specs=(P(), P(None, GRP), P(GRP, None)),
        check_vma=False,
    )
```

profile of v0, /device:TPU:6, one launch (start us, length us, event | category | flops | bytes accessed | tf_op | source)
XLA Modules:
  0.0 521.7 jit_solution(11916011583549820062)
XLA Ops:
  8.7 3.4 fusion.148
  13.4 54.5 %all-gather.3.cloned.1.call-done = bf16[2048,2048]{1,0:T(8,128)(2,1)} async-done(((bf16[128,2048]{1,0:T(8,128)(2,1)}), bf16[2048,2048]{1,0:T(8,128)(2,1)}) %all-gather.3.cloned.1.call-update) | async-done | bytes 8388624 | tf_op jit(solution)/shard_map/all_gather | solution.py:70
  67.9 5.9 %fusion.179 = f32[2048,256]{1,0:T(8,128)S(1)} fusion(bf16[2048,2048]{1,0:T(8,128)(2,1)} %all-gather.3.cloned.1.call-done, bf16[2048,256]{1,0:T(8,128)(2,1)S(1)} %copy-done), kind=kOutput, calls=%fused_computation.252 | convolution fusion | flops 2147483648 | bytes 11534336 | tf_op jit(solution)/shard_map/dot_general | solution.py:71
  75.1 32.5 %all_to_all.15 = f32[16,128,256]{2,1,0:T(8,128)S(1)} all-to-all(f32[16,128,256]{2,1,0:T(8,128)S(1)} %bitcast.55), channel_id=1, replica_groups=mesh['blk_0'=4,'blk_1'=2,'grp_0'=2,'grp_1'=4,'grp_2'=2] {'grp_0','grp_1'..., dimensions={0} | all-to-all | bytes 4194304 | tf_op jit(solution)/shard_map/all_to_all | solution.py:22
  108.0 19.1 %all_to_all.16 = bf16[16,128,256]{2,1,0:T(8,128)(2,1)S(1)} all-to-all(bf16[16,128,256]{2,1,0:T(8,128)(2,1)S(1)} %broadcast_in_dim.41), channel_id=1, replica_groups=mesh['blk_0'=4,'blk_1'=2,'grp_0'=2,'grp_1'=4,'grp_2'=2] {'grp_0','grp_1'..., dimensions={0} | all-to-all | bytes 2097152 | tf_op jit(solution)/shard_map/all_to_all | solution.py:34
  129.9 23.7 %collective-permute-done = bf16[2048,256]{1,0:T(8,128)(2,1)S(1)} collective-permute-done((bf16[2048,256]{1,0:T(8,128)(2,1)S(1)}, bf16[2048,256]{1,0:T(8,128)(2,1)S(1)}, u32[]{:S(2)}, u32[]{:S(2)}) %collective-permute-start) | collective-permute-done | bytes 1048608 | tf_op jit(solution)/shard_map/ppermute | solution.py:46
  155.6 23.7 %collective-permute-done.1 = bf16[2048,256]{1,0:T(8,128)(2,1)S(1)} collective-permute-done((bf16[2048,256]{1,0:T(8,128)(2,1)S(1)}, bf16[2048,256]{1,0:T(8,128)(2,1)S(1)}, u32[]{:S(2)}, u32[]{:S(2)}) %collective-permute-start.1) | collective-permute-done | bytes 1048608 | tf_op jit(solution)/shard_map/ppermute | solution.py:46
  181.5 23.8 %collective-permute-done.2 = bf16[2048,256]{1,0:T(8,128)(2,1)S(1)} collective-permute-done((bf16[2048,256]{1,0:T(8,128)(2,1)S(1)}, bf16[2048,256]{1,0:T(8,128)(2,1)S(1)}, u32[]{:S(2)}, u32[]{:S(2)}) %collective-permute-start.2) | collective-permute-done | bytes 1048608 | tf_op jit(solution)/shard_map/ppermute | solution.py:46
  207.3 23.0 %collective-permute-done.3 = bf16[2048,256]{1,0:T(8,128)(2,1)} collective-permute-done((bf16[2048,256]{1,0:T(8,128)(2,1)S(1)}, bf16[2048,256]{1,0:T(8,128)(2,1)}, u32[]{:S(2)}, u32[]{:S(2)}) %collective-permute-start.3) | collective-permute-done | bytes 1048608 | tf_op jit(solution)/shard_map/ppermute | solution.py:46
  232.5 21.3 %collective-permute-done.4 = bf16[2048,256]{1,0:T(8,128)(2,1)} collective-permute-done((bf16[2048,256]{1,0:T(8,128)(2,1)}, bf16[2048,256]{1,0:T(8,128)(2,1)}, u32[]{:S(2)}, u32[]{:S(2)}) %collective-permute-start.4) | collective-permute-done | bytes 1048608 | tf_op jit(solution)/shard_map/ppermute | solution.py:46
  253.8 3.5 collective-permute-start.5
  259.0 18.3 %collective-permute-done.5 = bf16[2048,256]{1,0:T(8,128)(2,1)S(1)} collective-permute-done((bf16[2048,256]{1,0:T(8,128)(2,1)}, bf16[2048,256]{1,0:T(8,128)(2,1)S(1)}, u32[]{:S(2)}, u32[]{:S(2)}) %collective-permute-start.5) | collective-permute-done | bytes 1048608 | tf_op jit(solution)/shard_map/ppermute | solution.py:46
  277.3 3.7 collective-permute-start.6
  285.5 13.3 %collective-permute-done.6 = bf16[2048,256]{1,0:T(8,128)(2,1)S(1)} collective-permute-done((bf16[2048,256]{1,0:T(8,128)(2,1)S(1)}, bf16[2048,256]{1,0:T(8,128)(2,1)S(1)}, u32[]{:S(2)}, u32[]{:S(2)}) %collective-permute-start.6) | collective-permute-done | bytes 1048608 | tf_op jit(solution)/shard_map/ppermute | solution.py:46
  302.6 44.5 %all-gather = f32[128,1,128]{2,1,0:T(1,128)S(1)} all-gather(f32[1,1,128]{2,1,0:T(1,128)S(1)} %bitcast.59), channel_id=1, replica_groups=mesh['blk_0'=4,'blk_1'=2,'grp_0'=2,'grp_1'=4,'grp_2'=2] {'blk_0','blk_1'..., dimensions={0}, use_global_device_ids=true | all-gather | bytes 66048 | tf_op jit(solution)/shard_map/all_gather | solution.py:109
  359.7 20.1 %all_to_all.17 = bf16[16,128,256]{2,1,0:T(8,128)(2,1)S(1)} all-to-all(bf16[16,128,256]{2,1,0:T(8,128)(2,1)S(1)} %broadcast_in_dim.42), channel_id=1, replica_groups=mesh['blk_0'=4,'blk_1'=2,'grp_0'=2,'grp_1'=4,'grp_2'=2] {'grp_0','grp_1'..., dimensions={0} | all-to-all | bytes 2097152 | tf_op jit(solution)/shard_map/all_to_all | solution.py:34
  381.4 9.3 %fusion.41 = f32[2048,256]{1,0:T(8,128)} fusion(bf16[2048,2048]{1,0:T(8,128)(2,1)} %all-gather.3.cloned.1.call-done, f32[2048,256]{1,0:T(8,128)} %copy-done.8, bf16[2048,256]{1,0:T(8,128)(2,1)S(1)} %bitcast.57, bf16[256,256]{1,0:T(8,128)(2,1)S(1)} %copy-done.6), kind=kOutput, calls=%fused_computation.114 | convolution fusion | flops 2426404864 | bytes 13762560 | tf_op jit(solution)/shard_map/dot_general | solution.py:143
  390.7 8.9 %psum.49 = f32[]{:T(128)} all-reduce(f32[]{:T(128)} %get-tuple-element.35), channel_id=1, replica_groups=mesh['blk_0'=4,'blk_1'=2,'grp_0'=2,'grp_1'=4,'grp_2'=2] {'blk_0'}, use_global_device_ids=true, to_apply=%region_19.20 | all-reduce | flops 1 | bytes 8 | tf_op jit(solution)/shard_map/psum | solution.py:51
  399.6 7.3 %psum.50 = f32[]{:T(128)} all-reduce(f32[]{:T(128)} %psum.49), channel_id=1, replica_groups=mesh['blk_0'=4,'blk_1'=2,'grp_0'=2,'grp_1'=4,'grp_2'=2] {'blk_1'}, use_global_device_ids=true, to_apply=%region_20.21 | all-reduce | flops 1 | bytes 8 | tf_op jit(solution)/shard_map/psum | solution.py:51
  406.8 5.7 %psum.51 = f32[]{:T(128)} all-reduce(f32[]{:T(128)} %psum.50), channel_id=1, replica_groups=mesh['blk_0'=4,'blk_1'=2,'grp_0'=2,'grp_1'=4,'grp_2'=2] {'grp_0'}, use_global_device_ids=true, to_apply=%region_21.22 | all-reduce | flops 1 | bytes 8 | tf_op jit(solution)/shard_map/psum | solution.py:51
  412.6 10.6 %psum.52 = f32[]{:T(128)} all-reduce(f32[]{:T(128)} %psum.51), channel_id=1, replica_groups=mesh['blk_0'=4,'blk_1'=2,'grp_0'=2,'grp_1'=4,'grp_2'=2] {'grp_1'}, use_global_device_ids=true, to_apply=%region_22.23 | all-reduce | flops 1 | bytes 8 | tf_op jit(solution)/shard_map/psum | solution.py:51
  423.2 3.1 psum.53
  426.9 83.0 %all-reduce.3.cloned.1.call-done = (f32[2048,256]{1,0:T(8,128)}, f32[256,256]{1,0:T(8,128)}) async-done(((f32[2048,256]{1,0:T(8,128)}, f32[256,256]{1,0:T(8,128)}), (f32[2048,256]{1,0:T(8,128)}, f32[256,256]{1,0:T(8,128)})) %all-reduce.3.cloned.1.call-update) | async-done | bytes 2359312 | tf_op jit(solution)/shard_map/psum | solution.py:146
  509.9 3.1 copy.16
  (73 shorter events, 40.3 us)
Async XLA Ops:
  7.2 60.7 %copy-start = (bf16[2048,256]{1,0:T(8,128)(2,1)S(1)}, bf16[2048,256]{1,0:T(8,128)(2,1)}, u32[]{:S(2)}) copy-start(bf16[2048,256]{1,0:T(8,128)(2,1)} %param.8) | copy-start | bytes 3145732
  7.2 60.7 %all-gather.3.cloned.1.call-start = ((), (), s32[]{:S(2)}) async-start(), calls=%async_computation.3 | async-start | bytes 8912896 | tf_op jit(solution)/shard_map/all_gather | solution.py:70
  13.3 60.4 %copy-start.6 = (bf16[256,256]{1,0:T(8,128)(2,1)S(1)}, bf16[256,256]{1,0:T(8,128)(2,1)}, u32[]{:S(2)}) copy-start(bf16[256,256]{1,0:T(8,128)(2,1)} %param.9) | copy-start | bytes 393220
  13.3 496.6 %all-reduce.3.cloned.1.call-start = ((), (), s32[]{:S(2)}) async-start(), calls=%async_computation.4 | async-start | bytes 4718592 | tf_op jit(solution)/shard_map/psum | solution.py:146
  73.7 1.3 copy-start.8
  127.1 26.6 %collective-permute-start = (bf16[2048,256]{1,0:T(8,128)(2,1)S(1)}, bf16[2048,256]{1,0:T(8,128)(2,1)S(1)}, u32[]{:S(2)}, u32[]{:S(2)}) collective-permute-start(bf16[2048,256]{1,0:T(8,128)(2,1)S(1)} %bitcast.51), channel_id=1, source_target_pairs={{112,0},{0,16},{16,32},{32,48},{48,64},{64,80},{80,96},{96,112},{1... | collective-permute-start | bytes 3145736 | tf_op jit(solution)/shard_map/ppermute | solution.py:46
  153.7 25.7 %collective-permute-start.1 = (bf16[2048,256]{1,0:T(8,128)(2,1)S(1)}, bf16[2048,256]{1,0:T(8,128)(2,1)S(1)}, u32[]{:S(2)}, u32[]{:S(2)}) collective-permute-start(bf16[2048,256]{1,0:T(8,128)(2,1)S(1)} %collective-permute-done), channel_id=1, source_target_pairs={{112,0},{0,16},{16,32},{32,48},{48,64},{64,80},{80,96},{96,112},{1... | collective-permute-start | bytes 3145736 | tf_op jit(solution)/shard_map/ppermute | solution.py:46
  179.4 1.1 copy-start.1
  180.4 24.8 %collective-permute-start.2 = (bf16[2048,256]{1,0:T(8,128)(2,1)S(1)}, bf16[2048,256]{1,0:T(8,128)(2,1)S(1)}, u32[]{:S(2)}, u32[]{:S(2)}) collective-permute-start(bf16[2048,256]{1,0:T(8,128)(2,1)S(1)} %collective-permute-done.1), channel_id=1, source_target_pairs={{112,0},{0,16},{16,32},{32,48},{48,64},{64,80},{80,96},{96,112},{1... | collective-permute-start | bytes 3145736 | tf_op jit(solution)/shard_map/ppermute | solution.py:46
  205.3 1.0 copy-start.3
  206.2 24.1 %collective-permute-start.3 = (bf16[2048,256]{1,0:T(8,128)(2,1)S(1)}, bf16[2048,256]{1,0:T(8,128)(2,1)}, u32[]{:S(2)}, u32[]{:S(2)}) collective-permute-start(bf16[2048,256]{1,0:T(8,128)(2,1)S(1)} %collective-permute-done.2), channel_id=1, source_target_pairs={{112,0},{0,16},{16,32},{32,48},{48,64},{64,80},{80,96},{96,112},{1... | collective-permute-start | bytes 3145736 | tf_op jit(solution)/shard_map/ppermute | solution.py:46
  230.3 23.4 %collective-permute-start.4 = (bf16[2048,256]{1,0:T(8,128)(2,1)}, bf16[2048,256]{1,0:T(8,128)(2,1)}, u32[]{:S(2)}, u32[]{:S(2)}) collective-permute-start(bf16[2048,256]{1,0:T(8,128)(2,1)} %collective-permute-done.3), channel_id=1, source_target_pairs={{112,0},{0,16},{16,32},{32,48},{48,64},{64,80},{80,96},{96,112},{1... | collective-permute-start | bytes 3145736 | tf_op jit(solution)/shard_map/ppermute | solution.py:46
  253.8 23.5 %collective-permute-start.5 = (bf16[2048,256]{1,0:T(8,128)(2,1)}, bf16[2048,256]{1,0:T(8,128)(2,1)S(1)}, u32[]{:S(2)}, u32[]{:S(2)}) collective-permute-start(bf16[2048,256]{1,0:T(8,128)(2,1)} %collective-permute-done.4), channel_id=1, source_target_pairs={{112,0},{0,16},{16,32},{32,48},{48,64},{64,80},{80,96},{96,112},{1... | collective-permute-start | bytes 3145736 | tf_op jit(solution)/shard_map/ppermute | solution.py:46
  257.3 1.2 copy-start.2
  257.8 23.3 %copy-start.4 = (bf16[2048,256]{1,0:T(8,128)(2,1)S(1)}, bf16[2048,256]{1,0:T(8,128)(2,1)}, u32[]{:S(2)}) copy-start(bf16[2048,256]{1,0:T(8,128)(2,1)} %copy-done.3) | copy-start | bytes 3145732
  277.3 21.4 %collective-permute-start.6 = (bf16[2048,256]{1,0:T(8,128)(2,1)S(1)}, bf16[2048,256]{1,0:T(8,128)(2,1)S(1)}, u32[]{:S(2)}, u32[]{:S(2)}) collective-permute-start(bf16[2048,256]{1,0:T(8,128)(2,1)S(1)} %collective-permute-done.5), channel_id=1, source_target_pairs={{112,0},{0,16},{16,32},{32,48},{48,64},{64,80},{80,96},{96,112},{1... | collective-permute-start | bytes 3145736 | tf_op jit(solution)/shard_map/ppermute | solution.py:46
  283.3 15.5 %copy-start.7 = (s32[128]{0:T(128)S(1)}, s32[128]{0:T(128)}, u32[]{:S(2)}) copy-start(s32[128]{0:T(128)} %param.7) | copy-start | bytes 1540
  359.5 20.3 %copy-start.9 = (f32[2048,256]{1,0:T(8,128)S(1)}, f32[2048,256]{1,0:T(8,128)}, u32[]{:S(2)}) copy-start(f32[2048,256]{1,0:T(8,128)} %copy-done.8) | copy-start | bytes 6291460
  509.9 3.1 copy-start.5
Sparse Core Ops, SparseCore 0:
  13.4 54.3 all-gather.2
  390.8 119.0 all-reduce.2
where the time goes:
time: 522 us
  waiting for transfers between devices  285 us (55%)
  blocking collectives  152 us (29%)
  matrix products  42.2 us (8%)
  starting transfers between devices  16.4 us (3%)
  between operations  16.1 us (3%)
  local copies, waits for them, and re-layouts  6.82 us (1%)
    ppermute x7, waiting for transfers between devices, shifted(): return lax.ppermute(block, axis, route)  147 us
    psum x1, waiting for transfers between devices, shards(): first_grad, second_grad = lax.psum((first_grad, second_grad), BLK)  83 us
    all_gather x1, waiting for transfers between devices, shards(): pooled_all = lax.all_gather(pooled, GRP, axis=0, tiled=True)  54.5 us
    all_gather x1, blocking collectives, shards(): every_norm = lax.all_gather(log_norm, BLK_GRP, axis=0, tiled=True)  44.5 us
    all_to_all x2, blocking collectives, from_everyone(): lax.all_to_all(jnp.broadcast_to(array[None], (peers, *array.shape)), axis...  39.2 us
    psum x5, blocking collectives, by_axis(): array = lax.psum(array, axis)  35.6 us
    all_to_all x1, blocking collectives, sent_and_summed(): lax.all_to_all(in_blocks(array, dim, peers), axis, 0, 0, tiled=True)  32.5 us
    ppermute x7, starting transfers between devices, shifted(): return lax.ppermute(block, axis, route)  16.3 us
  transfers between devices with their start and end apart: 9, of which 9 were waited for; matrix products, arithmetic and copies ran while one was open for 1% of the time, Pallas kernels for 0%

commit v1 on v0

--- a/solution.py
+++ b/solution.py
@@ -1,14 +1,27 @@
+import functools
 import jax
 import jax.numpy as jnp
 from jax import lax
 from jax.sharding import Mesh
 from jax.sharding import PartitionSpec as P
+from jax.lax import all_to_all, axis_size
 
 BLK = ("blk_0", "blk_1")
 GRP = ("grp_0", "grp_1", "grp_2")
 BLK_GRP = ("blk_0", "blk_1", "grp_0", "grp_1", "grp_2")
 logit_sharpness_divisor = 0.05
 score_top = 20.0
+
+
+def view_the_shelves(own_rows, net_axis):
+    response = jnp.concatenate(
+        all_to_all(jnp.stack([own_rows for _ in range(axis_size(net_axis))]), net_axis, 0, 0),
+        axis=0,
+    )
+    return response
+
+
+get_the_counts = functools.partial(view_the_shelves, net_axis=GRP)
 
 
 def in_blocks(array, dim, peers):
@@ -67,7 +80,7 @@
     )
     summed = jnp.einsum("rf,rfc->rc", frame_mask, frames, preferred_element_type=jnp.float32)
     pooled = (summed / counts[:, None].astype(jnp.float32)).astype(jnp.bfloat16)
-    pooled_all = lax.all_gather(pooled, GRP, axis=0, tiled=True)
+    pooled_all = get_the_counts(pooled)
     preact = jnp.dot(pooled_all, w_first, preferred_element_type=jnp.float32)
     hidden = jax.nn.gelu(preact).astype(jnp.bfloat16)
     raw_keys = sent_and_summed(

time: 522 us -> 568 us (1.088)
  blocking collectives: 152 us -> 251 us
  waiting for transfers between devices: 285 us -> 223 us
  starting transfers between devices: 16.4 us -> 24.4 us
    all_to_all x0 -> x1, blocking collectives: none -> 101 us  [view_the_shelves(): all_to_all(jnp.stack([own_rows for _ in range(axis_size(net_axis))]), net...]
    all_gather x1 -> x0, waiting for transfers between devices: 54.5 us -> none  [shards(): pooled_all = lax.all_gather(pooled, GRP, axis=0, tiled=True)]
    ppermute x7, starting transfers between devices: 16.3 us -> 24.4 us  [shifted(): return lax.ppermute(block, axis, route)]
    ppermute x7, waiting for transfers between devices: 147 us -> 140 us  [shifted(): return lax.ppermute(block, axis, route)]
  transfers between devices with their start and end apart: 9 -> 8, of which waited for: 9 -> 8; matrix products, arithmetic and copies ran while one was open for 1% -> 1% of each run, Pallas kernels for 0% -> 0%
where the time goes in v1:
time: 568 us; the launch traced here: 567 us
  blocking collectives  251 us (44%)
  waiting for transfers between devices  223 us (39%)
  matrix products  40.3 us (7%)
  starting transfers between devices  24.4 us (4%)
  between operations  16.1 us (3%)
  local copies, waits for them, and re-layouts  8.64 us (2%)
    ppermute x7, waiting for transfers between devices, shifted(): return lax.ppermute(block, axis, route)  140 us
    all_to_all x1, blocking collectives, view_the_shelves(): all_to_all(jnp.stack([own_rows for _ in range(axis_size(net_axis))]), net...  101 us
    psum x1, waiting for transfers between devices, shards(): first_grad, second_grad = lax.psum((first_grad, second_grad), BLK)  83 us
    all_gather x1, blocking collectives, shards(): every_norm = lax.all_gather(log_norm, BLK_GRP, axis=0, tiled=True)  45.6 us
    all_to_all x2, blocking collectives, from_everyone(): lax.all_to_all(jnp.broadcast_to(array[None], (peers, *array.shape)), axis...  39.1 us
    psum x5, blocking collectives, by_axis(): array = lax.psum(array, axis)  35.6 us
    all_to_all x1, blocking collectives, sent_and_summed(): lax.all_to_all(in_blocks(array, dim, peers), axis, 0, 0, tiled=True)  30.3 us
    ppermute x7, starting transfers between devices, shifted(): return lax.ppermute(block, axis, route)  24.4 us
  transfers between devices with their start and end apart: 8, of which 8 were waited for; matrix products, arithmetic and copies ran while one was open for 1% of the time, Pallas kernels for 0%

profile of v1, /device:TPU:6, one launch (start us, length us, event | category | flops | bytes accessed | tf_op | source)
XLA Modules:
  0.0 566.9 jit_solution(17816319701077877760)
XLA Ops:
  8.7 3.4 fusion.148
  13.6 100.8 %all_to_all.20 = bf16[16,128,2048]{2,1,0:T(8,128)(2,1)S(1)} all-to-all(bf16[16,128,2048]{2,1,0:T(8,128)(2,1)S(1)} %stack.2), channel_id=1, replica_groups=mesh['blk_0'=4,'blk_1'=2,'grp_0'=2,'grp_1'=4,'grp_2'=2] {'grp_0','grp_1'..., dimensions={0} | all-to-all | bytes 16777216 | tf_op jit(solution)/shard_map/all_to_all | solution.py:18
  118.9 30.3 %all_to_all.21 = f32[16,128,256]{2,1,0:T(8,128)S(1)} all-to-all(f32[16,128,256]{2,1,0:T(8,128)S(1)} %bitcast.58), channel_id=1, replica_groups=mesh['blk_0'=4,'blk_1'=2,'grp_0'=2,'grp_1'=4,'grp_2'=2] {'grp_0','grp_1'..., dimensions={0} | all-to-all | bytes 4194304 | tf_op jit(solution)/shard_map/all_to_all | solution.py:35
  149.7 19.1 %all_to_all.22 = bf16[16,128,256]{2,1,0:T(8,128)(2,1)S(1)} all-to-all(bf16[16,128,256]{2,1,0:T(8,128)(2,1)S(1)} %broadcast_in_dim.41), channel_id=1, replica_groups=mesh['blk_0'=4,'blk_1'=2,'grp_0'=2,'grp_1'=4,'grp_2'=2] {'grp_0','grp_1'..., dimensions={0} | all-to-all | bytes 2097152 | tf_op jit(solution)/shard_map/all_to_all | solution.py:47
  168.8 3.6 collective-permute-start
  172.4 23.0 %collective-permute-done = bf16[2048,256]{1,0:T(8,128)(2,1)S(1)} collective-permute-done((bf16[2048,256]{1,0:T(8,128)(2,1)S(1)}, bf16[2048,256]{1,0:T(8,128)(2,1)S(1)}, u32[]{:S(2)}, u32[]{:S(2)}) %collective-permute-start) | collective-permute-done | bytes 1048608 | tf_op jit(solution)/shard_map/ppermute | solution.py:59
  198.0 23.0 %collective-permute-done.1 = bf16[2048,256]{1,0:T(8,128)(2,1)S(1)} collective-permute-done((bf16[2048,256]{1,0:T(8,128)(2,1)S(1)}, bf16[2048,256]{1,0:T(8,128)(2,1)S(1)}, u32[]{:S(2)}, u32[]{:S(2)}) %collective-permute-start.1) | collective-permute-done | bytes 1048608 | tf_op jit(solution)/shard_map/ppermute | solution.py:59
  223.9 23.1 %collective-permute-done.2 = bf16[2048,256]{1,0:T(8,128)(2,1)S(1)} collective-permute-done((bf16[2048,256]{1,0:T(8,128)(2,1)S(1)}, bf16[2048,256]{1,0:T(8,128)(2,1)S(1)}, u32[]{:S(2)}, u32[]{:S(2)}) %collective-permute-start.2) | collective-permute-done | bytes 1048608 | tf_op jit(solution)/shard_map/ppermute | solution.py:59
  249.9 22.1 %collective-permute-done.3 = bf16[2048,256]{1,0:T(8,128)(2,1)} collective-permute-done((bf16[2048,256]{1,0:T(8,128)(2,1)S(1)}, bf16[2048,256]{1,0:T(8,128)(2,1)}, u32[]{:S(2)}, u32[]{:S(2)}) %collective-permute-start.3) | collective-permute-done | bytes 1048608 | tf_op jit(solution)/shard_map/ppermute | solution.py:59
  272.0 3.3 collective-permute-start.4
  275.4 20.1 %collective-permute-done.4 = bf16[2048,256]{1,0:T(8,128)(2,1)} collective-permute-done((bf16[2048,256]{1,0:T(8,128)(2,1)}, bf16[2048,256]{1,0:T(8,128)(2,1)}, u32[]{:S(2)}, u32[]{:S(2)}) %collective-permute-start.4) | collective-permute-done | bytes 1048608 | tf_op jit(solution)/shard_map/ppermute | solution.py:59
  295.5 4.9 collective-permute-start.5
  302.1 16.3 %collective-permute-done.5 = bf16[2048,256]{1,0:T(8,128)(2,1)S(1)} collective-permute-done((bf16[2048,256]{1,0:T(8,128)(2,1)}, bf16[2048,256]{1,0:T(8,128)(2,1)S(1)}, u32[]{:S(2)}, u32[]{:S(2)}) %collective-permute-start.5) | collective-permute-done | bytes 1048608 | tf_op jit(solution)/shard_map/ppermute | solution.py:59
  318.4 6.1 %collective-permute-start.6 = (bf16[2048,256]{1,0:T(8,128)(2,1)S(1)}, bf16[2048,256]{1,0:T(8,128)(2,1)S(1)}, u32[]{:S(2)}, u32[]{:S(2)}) collective-permute-start(bf16[2048,256]{1,0:T(8,128)(2,1)S(1)} %collective-permute-done.5), channel_id=1, source_target_pairs={{112,0},{0,16},{16,32},{32,48},{48,64},{64,80},{80,96},{96,112},{1... | collective-permute-start | bytes 3145736 | tf_op jit(solution)/shard_map/ppermute | solution.py:59
  328.9 12.4 %collective-permute-done.6 = bf16[2048,256]{1,0:T(8,128)(2,1)S(1)} collective-permute-done((bf16[2048,256]{1,0:T(8,128)(2,1)S(1)}, bf16[2048,256]{1,0:T(8,128)(2,1)S(1)}, u32[]{:S(2)}, u32[]{:S(2)}) %collective-permute-start.6) | collective-permute-done | bytes 1048608 | tf_op jit(solution)/shard_map/ppermute | solution.py:59
  345.2 45.6 %all-gather = f32[128,1,128]{2,1,0:T(1,128)S(1)} all-gather(f32[1,1,128]{2,1,0:T(1,128)S(1)} %bitcast.62), channel_id=1, replica_groups=mesh['blk_0'=4,'blk_1'=2,'grp_0'=2,'grp_1'=4,'grp_2'=2] {'blk_0','blk_1'..., dimensions={0}, use_global_device_ids=true | all-gather | bytes 66048 | tf_op jit(solution)/shard_map/all_gather | solution.py:122
  403.4 20.0 %all_to_all.23 = bf16[16,128,256]{2,1,0:T(8,128)(2,1)S(1)} all-to-all(bf16[16,128,256]{2,1,0:T(8,128)(2,1)S(1)} %broadcast_in_dim.42), channel_id=1, replica_groups=mesh['blk_0'=4,'blk_1'=2,'grp_0'=2,'grp_1'=4,'grp_2'=2] {'grp_0','grp_1'..., dimensions={0} | all-to-all | bytes 2097152 | tf_op jit(solution)/shard_map/all_to_all | solution.py:47
  423.4 9.3 %fusion.41 = f32[2048,256]{1,0:T(8,128)} fusion(bf16[2048,2048]{1,0:T(8,128)(2,1)} %bitcast.53, f32[2048,256]{1,0:T(8,128)} %copy-done.9, bf16[2048,256]{1,0:T(8,128)(2,1)S(1)} %bitcast.59, bf16[256,256]{1,0:T(8,128)(2,1)S(1)} %copy-done.7), kind=kOutput, calls=%fused_computation.114 | convolution fusion | flops 2426404864 | bytes 13762560 | tf_op jit(solution)/shard_map/dot_general | solution.py:156
  432.7 3.1 fusion.174
  435.8 8.9 %psum.49 = f32[]{:T(128)} all-reduce(f32[]{:T(128)} %get-tuple-element.35), channel_id=1, replica_groups=mesh['blk_0'=4,'blk_1'=2,'grp_0'=2,'grp_1'=4,'grp_2'=2] {'blk_0'}, use_global_device_ids=true, to_apply=%region_19.20 | all-reduce | flops 1 | bytes 8 | tf_op jit(solution)/shard_map/psum | solution.py:64
  444.7 7.3 %psum.50 = f32[]{:T(128)} all-reduce(f32[]{:T(128)} %psum.49), channel_id=1, replica_groups=mesh['blk_0'=4,'blk_1'=2,'grp_0'=2,'grp_1'=4,'grp_2'=2] {'blk_1'}, use_global_device_ids=true, to_apply=%region_20.21 | all-reduce | flops 1 | bytes 8 | tf_op jit(solution)/shard_map/psum | solution.py:64
  452.0 5.7 %psum.51 = f32[]{:T(128)} all-reduce(f32[]{:T(128)} %psum.50), channel_id=1, replica_groups=mesh['blk_0'=4,'blk_1'=2,'grp_0'=2,'grp_1'=4,'grp_2'=2] {'grp_0'}, use_global_device_ids=true, to_apply=%region_21.22 | all-reduce | flops 1 | bytes 8 | tf_op jit(solution)/shard_map/psum | solution.py:64
  457.7 10.6 %psum.52 = f32[]{:T(128)} all-reduce(f32[]{:T(128)} %psum.51), channel_id=1, replica_groups=mesh['blk_0'=4,'blk_1'=2,'grp_0'=2,'grp_1'=4,'grp_2'=2] {'grp_1'}, use_global_device_ids=true, to_apply=%region_22.23 | all-reduce | flops 1 | bytes 8 | tf_op jit(solution)/shard_map/psum | solution.py:64
  472.1 83.0 %all-reduce.3.cloned.1.call-done = (f32[2048,256]{1,0:T(8,128)}, f32[256,256]{1,0:T(8,128)}) async-done(((f32[2048,256]{1,0:T(8,128)}, f32[256,256]{1,0:T(8,128)}), (f32[2048,256]{1,0:T(8,128)}, f32[256,256]{1,0:T(8,128)})) %all-reduce.3.cloned.1.call-update) | async-done | bytes 2359312 | tf_op jit(solution)/shard_map/psum | solution.py:159
  (72 shorter events, 45.6 us)
Async XLA Ops:
  7.2 107.2 %copy-start = (bf16[2048,256]{1,0:T(8,128)(2,1)S(1)}, bf16[2048,256]{1,0:T(8,128)(2,1)}, u32[]{:S(2)}) copy-start(bf16[2048,256]{1,0:T(8,128)(2,1)} %param.8) | copy-start | bytes 3145732
  7.2 547.9 %all-reduce.3.cloned.1.call-start = ((), (), s32[]{:S(2)}) async-start(), calls=%async_computation.4 | async-start | bytes 4718592 | tf_op jit(solution)/shard_map/psum | solution.py:159
  114.4 3.2 copy-start.1
  114.4 3.2 copy-start.7
  117.6 1.3 copy-start.9
  168.8 26.6 %collective-permute-start = (bf16[2048,256]{1,0:T(8,128)(2,1)S(1)}, bf16[2048,256]{1,0:T(8,128)(2,1)S(1)}, u32[]{:S(2)}, u32[]{:S(2)}) collective-permute-start(bf16[2048,256]{1,0:T(8,128)(2,1)S(1)} %bitcast.54), channel_id=1, source_target_pairs={{112,0},{0,16},{16,32},{32,48},{48,64},{64,80},{80,96},{96,112},{1... | collective-permute-start | bytes 3145736 | tf_op jit(solution)/shard_map/ppermute | solution.py:59
  195.3 25.7 %collective-permute-start.1 = (bf16[2048,256]{1,0:T(8,128)(2,1)S(1)}, bf16[2048,256]{1,0:T(8,128)(2,1)S(1)}, u32[]{:S(2)}, u32[]{:S(2)}) collective-permute-start(bf16[2048,256]{1,0:T(8,128)(2,1)S(1)} %collective-permute-done), channel_id=1, source_target_pairs={{112,0},{0,16},{16,32},{32,48},{48,64},{64,80},{80,96},{96,112},{1... | collective-permute-start | bytes 3145736 | tf_op jit(solution)/shard_map/ppermute | solution.py:59
  221.0 1.1 copy-start.2
  222.1 24.8 %collective-permute-start.2 = (bf16[2048,256]{1,0:T(8,128)(2,1)S(1)}, bf16[2048,256]{1,0:T(8,128)(2,1)S(1)}, u32[]{:S(2)}, u32[]{:S(2)}) collective-permute-start(bf16[2048,256]{1,0:T(8,128)(2,1)S(1)} %collective-permute-done.1), channel_id=1, source_target_pairs={{112,0},{0,16},{16,32},{32,48},{48,64},{64,80},{80,96},{96,112},{1... | collective-permute-start | bytes 3145736 | tf_op jit(solution)/shard_map/ppermute | solution.py:59
  246.9 1.0 copy-start.4
  247.9 24.1 %collective-permute-start.3 = (bf16[2048,256]{1,0:T(8,128)(2,1)S(1)}, bf16[2048,256]{1,0:T(8,128)(2,1)}, u32[]{:S(2)}, u32[]{:S(2)}) collective-permute-start(bf16[2048,256]{1,0:T(8,128)(2,1)S(1)} %collective-permute-done.2), channel_id=1, source_target_pairs={{112,0},{0,16},{16,32},{32,48},{48,64},{64,80},{80,96},{96,112},{1... | collective-permute-start | bytes 3145736 | tf_op jit(solution)/shard_map/ppermute | solution.py:59
  272.0 23.4 %collective-permute-start.4 = (bf16[2048,256]{1,0:T(8,128)(2,1)}, bf16[2048,256]{1,0:T(8,128)(2,1)}, u32[]{:S(2)}, u32[]{:S(2)}) collective-permute-start(bf16[2048,256]{1,0:T(8,128)(2,1)} %collective-permute-done.3), channel_id=1, source_target_pairs={{112,0},{0,16},{16,32},{32,48},{48,64},{64,80},{80,96},{96,112},{1... | collective-permute-start | bytes 3145736 | tf_op jit(solution)/shard_map/ppermute | solution.py:59
  295.5 22.9 %collective-permute-start.5 = (bf16[2048,256]{1,0:T(8,128)(2,1)}, bf16[2048,256]{1,0:T(8,128)(2,1)S(1)}, u32[]{:S(2)}, u32[]{:S(2)}) collective-permute-start(bf16[2048,256]{1,0:T(8,128)(2,1)} %collective-permute-done.4), channel_id=1, source_target_pairs={{112,0},{0,16},{16,32},{32,48},{48,64},{64,80},{80,96},{96,112},{1... | collective-permute-start | bytes 3145736 | tf_op jit(solution)/shard_map/ppermute | solution.py:59
  300.4 1.2 copy-start.3
  300.9 23.6 %copy-start.5 = (bf16[2048,256]{1,0:T(8,128)(2,1)S(1)}, bf16[2048,256]{1,0:T(8,128)(2,1)}, u32[]{:S(2)}) copy-start(bf16[2048,256]{1,0:T(8,128)(2,1)} %copy-done.4) | copy-start | bytes 3145732
  318.4 22.9 %collective-permute-start.6 = (bf16[2048,256]{1,0:T(8,128)(2,1)S(1)}, bf16[2048,256]{1,0:T(8,128)(2,1)S(1)}, u32[]{:S(2)}, u32[]{:S(2)}) collective-permute-start(bf16[2048,256]{1,0:T(8,128)(2,1)S(1)} %collective-permute-done.5), channel_id=1, source_target_pairs={{112,0},{0,16},{16,32},{32,48},{48,64},{64,80},{80,96},{96,112},{1... | collective-permute-start | bytes 3145736 | tf_op jit(solution)/shard_map/ppermute | solution.py:59
  326.7 14.6 %copy-start.8 = (s32[128]{0:T(128)S(1)}, s32[128]{0:T(128)}, u32[]{:S(2)}) copy-start(s32[128]{0:T(128)} %param.7) | copy-start | bytes 1540
  555.1 3.1 copy-start.6
Sparse Core Ops, SparseCore 0:
  435.9 119.0 all-reduce.2
